TPU v7x, 32 devices: a whole 2x2x4 slice. The times are simulated.
32 devices in a mesh: row: 8 (over z, core), col: 4 (over y, x).
Axes of the slice: x: 2, y: 2, z: 4, core: 2. Of those that a mesh axis runs over, the one named last changes fastest.
Arguments:
- tokens: bfloat16 [512, 4096], P(None, 'col'), may hold values from -6 to 6
- w_gate: bfloat16 [4096, 10240], P('col', 'row'), may hold values from -0.09375 to 0.09375
- w_up: bfloat16 [4096, 10240], P('col', 'row'), may hold values from -0.09375 to 0.09375
- w_down: bfloat16 [10240, 4096], P('row', 'col'), may hold values from -0.0625 to 0.0625
Outputs:
- result: bfloat16 [512, 4096], P('row', 'col')
All inputs are finite; a program needn't handle non-finite values.
Results may differ from a plain program's by a relative error of at most 0.025.
Values may be sent and summed in bfloat16 or wider, within the bound.
A program may use at most 64 MiB of HBM per device.

v0:
```python
import jax
import jax.numpy as jnp
from jax import lax
from jax.sharding import PartitionSpec as P


def activate(summed, hidden_width):
    pre_gate = summed[:, :hidden_width]
    pre_up = summed[:, hidden_width:]
    return (jax.nn.gelu(pre_gate, approximate=True) * pre_up).astype(jnp.bfloat16)


def local(tokens, w_gate, w_up, w_down):
    joined = jnp.concatenate([w_gate, w_up], axis=1)
    hidden_width = w_gate.shape[1]
    summed = lax.psum_scatter(
        jnp.dot(tokens, joined, preferred_element_type=jnp.float32).astype(jnp.bfloat16),
        "col",
        scatter_dimension=0,
        tiled=True,
    ).astype(jnp.float32)
    hidden = activate(summed, hidden_width)
    hidden_all = lax.all_gather(hidden, "col", axis=0, tiled=True)
    result = lax.psum_scatter(
        jnp.dot(hidden_all, w_down, preferred_element_type=jnp.float32),
        "row",
        scatter_dimension=0,
        tiled=True,
    )
    return result.astype(jnp.bfloat16)


def solution(mesh):
    in_specs = (P(None, "col"), P("col", "row"), P("col", "row"), P("row", "col"))
    out_specs = P("row", "col")
    return jax.shard_map(local, mesh=mesh, in_specs=in_specs, out_specs=out_specs, check_vma=False)
```

profile of v0, /device:TPU:0, one launch (start us, length us, event | category | flops | bytes accessed | tf_op | source)
XLA Modules:
  0.0 140.5 jit_solution(11129472664520844137)
XLA Ops:
  6.5 0.0 copy-start
  6.5 0.0 reduce-scatter.7.cloned.1.call-start
  6.5 7.4 %fusion.7 = bf16[512,2560]{0,1:T(8,128)(2,1)} fusion(bf16[512,1024]{1,0:T(8,128)(2,1)} %param.4, bf16[1024,1280]{1,0:T(8,128)(2,1)} %param.6, bf16[1024,1280]{1,0:T(8,128)(2,1)} %param.5), kind=kOutput, calls=%fused_computation.5 | convolution fusion | flops 2696151040 | bytes 8912896 | tf_op jit(solution)/shard_map/dot_general | solution.py:17
  13.9 4.4 %copy.5 = bf16[512,2560]{1,0:T(8,128)(2,1)} copy(bf16[512,2560]{0,1:T(8,128)(2,1)} %fusion.7) | data formatting | bytes 5242880
  18.3 0.0 reduce-scatter.7.cloned.1.call-update
  18.3 0.0 all-gather.2.cloned.1.call-start
  18.4 42.4 %reduce-scatter.7.cloned.1.call-done = bf16[128,2560]{1,0:T(8,128)(2,1)} async-done(((bf16[512,2560]{1,0:T(8,128)(2,1)}), bf16[128,2560]{1,0:T(8,128)(2,1)}) %reduce-scatter.7.cloned.1.call-update) | async-done | bytes 655376
  60.8 1.4 %copy.6 = bf16[128,2560]{0,1:T(8,128)(2,1)S(1)} copy(bf16[128,2560]{1,0:T(8,128)(2,1)} %reduce-scatter.7.cloned.1.call-done) | data formatting | bytes 1310720
  62.2 0.1 convert_element_type.17
  62.3 1.0 fusion.18
  63.2 0.0 all-gather.2.cloned.1.call-update
  63.3 0.0 reduce-scatter.5.cloned.1.call-start
  63.3 28.6 %all-gather.2.cloned.1.call-done = bf16[512,1280]{0,1:T(8,128)(2,1)} async-done(((bf16[128,1280]{0,1:T(8,128)(2,1)}), bf16[512,1280]{0,1:T(8,128)(2,1)}) %all-gather.2.cloned.1.call-update) | async-done | bytes 1310736 | tf_op jit(solution)/shard_map/all_gather | solution.py:23
  92.0 0.0 copy-done
  92.0 4.2 %fusion.20 = f32[512,1024]{1,0:T(8,128)} fusion(bf16[512,1280]{0,1:T(8,128)(2,1)} %all-gather.2.cloned.1.call-done, bf16[1280,1024]{1,0:T(8,128)(2,1)S(1)} %copy-done), kind=kOutput, calls=%fused_computation.17 | convolution fusion | flops 1342177280 | bytes 6029312 | tf_op jit(solution)/shard_map/dot_general | solution.py:25
  96.1 0.0 reduce-scatter.5.cloned.1.call-update
  96.2 36.2 %reduce-scatter.5.cloned.1.call-done = f32[64,1024]{1,0:T(8,128)} async-done(((f32[512,1024]{1,0:T(8,128)}), f32[64,1024]{1,0:T(8,128)}) %reduce-scatter.5.cloned.1.call-update) | async-done | bytes 262160 | tf_op jit(solution)/shard_map/reduce_scatter | solution.py:24
  132.3 1.6 %convert_element_type.19 = bf16[64,1024]{1,0:T(8,128)(2,1)} convert(f32[64,1024]{1,0:T(8,128)} %reduce-scatter.5.cloned.1.call-done) | non-fusion elementwise | flops 65536 | bytes 393216 | tf_op jit(solution)/shard_map/convert_element_type | solution.py:30
Async XLA Ops:
  6.5 85.4 %copy-start = (bf16[1280,1024]{1,0:T(8,128)(2,1)S(1)}, bf16[1280,1024]{1,0:T(8,128)(2,1)}, u32[]{:S(2)}) copy-start(bf16[1280,1024]{1,0:T(8,128)(2,1)} %param.7) | copy-start | bytes 7864324
  6.5 54.2 %reduce-scatter.7.cloned.1.call-start = ((), (), s32[]{:S(2)}) async-start(), calls=%async_computation.4 | async-start | bytes 3276800
  18.3 73.6 %all-gather.2.cloned.1.call-start = ((), (), s32[]{:S(2)}) async-start(), calls=%async_computation.2 | async-start | bytes 1638400 | tf_op jit(solution)/shard_map/all_gather | solution.py:23
  63.3 69.1 %reduce-scatter.5.cloned.1.call-start = ((), (), s32[]{:S(2)}) async-start(), calls=%async_computation.3 | async-start | bytes 2359296 | tf_op jit(solution)/shard_map/reduce_scatter | solution.py:24
Sparse Core Ops, SparseCore 0:
  18.5 42.2 reduce-scatter.6
  63.4 28.5 all-gather.1
  96.3 36.0 reduce-scatter.4
where the time goes:
time: 141 us; the launch traced here: 140 us
  waiting for transfers between devices  107 us (76%)
  between operations  13.1 us (9%)
  matrix products  11.6 us (8%)
  local copies, waits for them, and re-layouts  5.79 us (4%)
  other arithmetic  2.66 us (2%)
    unnamed x4, waiting for transfers between devices  42.4 us
    reduce_scatter x1, waiting for transfers between devices, local(): lax.psum_scatter(jnp.dot(hidden_all, w_down, preferred_element_type=jnp.f...  36.2 us
    all_gather x1, waiting for transfers between devices, local(): hidden_all = lax.all_gather(hidden, 'col', axis=0, tiled=True)  28.6 us
    dot_general x1, matrix products, local(): jnp.dot(tokens, joined, preferred_element_type=jnp.float32)  7.39 us
    unnamed x4, local copies, waits for them, and re-layouts  5.79 us
    dot_general x1, matrix products, local(): jnp.dot(hidden_all, w_down, preferred_element_type=jnp.float32)  4.18 us
  transfers between devices with their start and end apart: 3, of which 3 were waited for; matrix products, arithmetic and copies ran while one was open for 0% of the time, Pallas kernels for 0%

commit v1 on v0

v1 whole, which is shorter than its diff:
```python
import functools

import jax
import jax.numpy as jnp
from jax import lax
from jax.experimental import pallas as pl
from jax.experimental.pallas import tpu as pltpu
from jax.sharding import PartitionSpec as P

MESH = pl.DeviceIdType.MESH
PIECE = 16
TILE = 256


def activate(pre_gate, pre_up):
    return (jax.nn.gelu(pre_gate, approximate=True) * pre_up).astype(jnp.bfloat16)


def plain(tokens, w_gate, w_up, w_down):
    joined = jnp.concatenate([w_gate, w_up], axis=1)
    hidden_width = w_gate.shape[1]
    summed = lax.psum_scatter(
        jnp.dot(tokens, joined, preferred_element_type=jnp.float32).astype(jnp.bfloat16),
        "col",
        scatter_dimension=0,
        tiled=True,
    ).astype(jnp.float32)
    hidden = activate(summed[:, :hidden_width], summed[:, hidden_width:])
    hidden_all = lax.all_gather(hidden, "col", axis=0, tiled=True)
    result = lax.psum_scatter(
        jnp.dot(hidden_all, w_down, preferred_element_type=jnp.float32),
        "row",
        scatter_dimension=0,
        tiled=True,
    )
    return result.astype(jnp.bfloat16)


def kernel(
    n_row, chunks, tok_hbm, wg_hbm, wu_hbm, wd_hbm, out_ref,
    tok, w1, wd, s1, own, r1, s2, r2, hid, part, part16, c1r, c2s, c2r,
    load_sem, send1, recv1, send2, recv2, send3, recv3, send4, recv4, send5, recv5, send6, recv6,
):
    row, col = lax.axis_index("row"), lax.axis_index("col")
    y, x = col // 2, col % 2
    z, core = row // 2, row % 2
    n_z = n_row // 2
    half = w1.shape[2] // 2
    x_peer = (row, 2 * y + 1 - x)
    y_peer = (row, 2 * (1 - y) + x)
    core_peer = (2 * z + 1 - core, col)
    z_peers = [(2 * ((z + d) % n_z) + core, col) for d in range(1, n_z)]
    first_peer, second_peer = (x_peer, y_peer), (y_peer, x_peer)
    first_at, second_at = (x, y), (y, x)

    loads = [pltpu.make_async_copy(tok_hbm, tok, load_sem.at[0])]
    for mode in range(2):
        for k, w_hbm in enumerate((wg_hbm, wu_hbm)):
            loads.append(pltpu.make_async_copy(
                w_hbm.at[:, pl.ds(mode * half, half)],
                w1.at[mode, :, pl.ds(k * half, half)],
                load_sem.at[1 + 2 * mode + k],
            ))
    loads.append(pltpu.make_async_copy(wd_hbm, wd, load_sem.at[5]))
    for load in loads:
        load.start()

    barrier = pltpu.get_barrier_semaphore()
    peers = [x_peer, y_peer, core_peer] + z_peers
    for peer in peers:
        pl.semaphore_signal(barrier, inc=1, device_id=peer, device_id_type=MESH)

    def remote(src, dst, send_sem, recv_sem, peer):
        return pltpu.make_async_remote_copy(
            src_ref=src, dst_ref=dst, send_sem=send_sem, recv_sem=recv_sem, device_id=peer, device_id_type=MESH)

    def copy_s1(m, i):
        return remote(s1.at[m, i], r1.at[m, i], send1.at[m, i], recv1.at[m, i], first_peer[m])

    def copy_s2(m, i):
        return remote(s2.at[m, i], r2.at[m, i], send2.at[m, i], recv2.at[m, i], second_peer[m])

    def copy_g1(m, i):
        ref = hid.at[m, i, first_at[m], second_at[m]]
        return remote(ref, ref, send3.at[m, i], recv3.at[m, i], second_peer[m])

    def copy_g2(m, i):
        ref = hid.at[m, i, first_at[m]]
        return remote(ref, ref, send4.at[m, i], recv4.at[m, i], first_peer[m])

    def copy_c1(i):
        return remote(part16.at[i, 1 - core], c1r.at[i], send5.at[i], recv5.at[i], core_peer)

    def copy_c2(i, d):
        return remote(c2s.at[i, (z + d) % n_z], c2r.at[i, d - 1], send6.at[i, d - 1], recv6.at[i, d - 1], z_peers[d - 1])

    def product(m, mine, dst):
        at = first_at[m] if mine else 1 - first_at[m]
        rows = tok[:, at] if m == 0 else tok[at]
        rows = rows.reshape(-1, rows.shape[-1])

        @pl.loop(0, w1.shape[2] // TILE)
        def _(t):
            columns = pl.ds(pl.multiple_of(t * TILE, TILE), TILE)
            out = jnp.dot(rows, w1[m, :, columns], preferred_element_type=jnp.float32).astype(jnp.bfloat16)
            out = out.reshape(2, n_row // 4, chunks, PIECE, TILE)
            for i in range(chunks):
                dst[m, i, :, :, :, columns] = out[:, :, i]

    def f32(v):
        return v.astype(jnp.float32)

    def do_s1(i):
        for m in range(2):
            copy_s1(m, i).start()

    def do_s2(i):
        for m in range(2):
            copy_s1(m, i).wait_recv()
            at = 1 - second_at[m]
            s2[m, i] = (f32(own[m, i, at]) + f32(r1[m, i, at])).astype(jnp.bfloat16)
            copy_s2(m, i).start()

    def do_g1(i):
        for m in range(2):
            copy_s2(m, i).wait_recv()
            at = second_at[m]
            pre = f32(own[m, i, at]) + f32(r1[m, i, at]) + f32(r2[m, i])
            hid[m, i, first_at[m], at] = activate(pre[..., :half], pre[..., half:])
            copy_g1(m, i).start()

    def do_g2(i):
        for m in range(2):
            copy_g1(m, i).wait_recv()
            copy_g2(m, i).start()

    def do_c1(i):
        for m in range(2):
            copy_g2(m, i).wait_recv()
        rows = n_row // 4 * PIECE
        quarters = [
            jnp.concatenate([hid[0, i, b, a].reshape(rows, half), hid[1, i, a, b].reshape(rows, half)], axis=1)
            for a in range(2) for b in range(2)
        ]
        hidden = jnp.concatenate(quarters, axis=0)
        for t in range(wd.shape[1] // TILE):
            columns = slice(t * TILE, (t + 1) * TILE)
            out = jnp.dot(hidden, wd[:, columns], preferred_element_type=jnp.float32)
            out = out.reshape(n_z, 2, PIECE, TILE)
            for c in range(2):
                part[i, c, :, :, columns] = out[:, c]
                part16[i, c, :, :, columns] = out[:, c].astype(jnp.bfloat16)
        copy_c1(i).start()

    def do_c2(i):
        copy_c1(i).wait_recv()
        c2s[i] = (part[i, core] + f32(c1r[i])).astype(jnp.bfloat16)
        for d in range(1, n_z):
            copy_c2(i, d).start()

    def do_out(i):
        total = part[i, core, z] + f32(c1r[i, z])
        for d in range(1, n_z):
            copy_c2(i, d).wait_recv()
            total = total + f32(c2r[i, d - 1])
        out_ref[pl.ds(i * PIECE, PIECE), :] = total.astype(jnp.bfloat16)

    for load in loads[:3]:
        load.wait()
    product(0, False, s1)
    pl.semaphore_wait(barrier, len(peers))
    ahead = min(2, chunks)
    for i in range(ahead):
        copy_s1(0, i).start()
    for load in loads[3:5]:
        load.wait()
    product(1, False, s1)
    for i in range(ahead):
        copy_s1(1, i).start()
    product(0, True, own)
    product(1, True, own)
    loads[5].wait()

    for k in range(chunks + 6):
        for stage, late in ((do_s2, 0), (do_g1, 1), (do_s1, -2), (do_g2, 2), (do_c2, 4), (do_c1, 3), (do_out, 6)):
            i = k - late
            if 0 <= i < chunks and (stage is not do_s1 or i >= ahead):
                stage(i)

    for i in range(chunks):
        for m in range(2):
            for copy in (copy_s1, copy_s2, copy_g1, copy_g2):
                copy(m, i).wait_send()
        copy_c1(i).wait_send()
        for d in range(1, n_z):
            copy_c2(i, d).wait_send()


def fused(n_row, tokens, w_gate, w_up, w_down):
    n_tok, depth = tokens.shape
    width, features = w_down.shape
    per_row = n_tok // n_row
    chunks = per_row // PIECE
    n_z, blocks, half = n_row // 2, n_row // 4, width // 2
    bf16, dma = jnp.bfloat16, pltpu.SemaphoreType.DMA
    pair = [dma((2, chunks))] * 8
    return pl.pallas_call(
        functools.partial(kernel, n_row, chunks),
        out_shape=jax.ShapeDtypeStruct((per_row, features), bf16),
        in_specs=[pl.BlockSpec(memory_space=pl.ANY)] * 4,
        out_specs=pl.BlockSpec(memory_space=pltpu.VMEM),
        scratch_shapes=[
            pltpu.VMEM((2, 2, n_tok // 4, depth), bf16),
            pltpu.VMEM((2, depth, width), bf16),
            pltpu.VMEM((width, features), bf16),
            pltpu.VMEM((2, chunks, 2, blocks, PIECE, width), bf16),
            pltpu.VMEM((2, chunks, 2, blocks, PIECE, width), bf16),
            pltpu.VMEM((2, chunks, 2, blocks, PIECE, width), bf16),
            pltpu.VMEM((2, chunks, blocks, PIECE, width), bf16),
            pltpu.VMEM((2, chunks, blocks, PIECE, width), bf16),
            pltpu.VMEM((2, chunks, 2, 2, blocks, PIECE, half), bf16),
            pltpu.VMEM((chunks, 2, n_z, PIECE, features), jnp.float32),
            pltpu.VMEM((chunks, 2, n_z, PIECE, features), bf16),
            pltpu.VMEM((chunks, n_z, PIECE, features), bf16),
            pltpu.VMEM((chunks, n_z, PIECE, features), bf16),
            pltpu.VMEM((chunks, n_z - 1, PIECE, features), bf16),
            dma((6,)),
            *pair,
            dma((chunks,)), dma((chunks,)),
            dma((chunks, n_z - 1)), dma((chunks, n_z - 1)),
        ],
        compiler_params=pltpu.CompilerParams(
            collective_id=0, has_side_effects=True, vmem_limit_bytes=48 * 1024 * 1024
        ),
    )(tokens.reshape(2, 2, n_tok // 4, depth), w_gate, w_up, w_down)


def solution(mesh):
    n_row, n_col = mesh.shape["row"], mesh.shape["col"]

    def local(tokens, w_gate, w_up, w_down):
        width, features = w_down.shape
        fits = (
            n_col == 4
            and n_row % 4 == 0
            and n_row <= 16
            and tokens.shape[0] % (n_row * PIECE) == 0
            and tokens.shape[0] // (n_row * PIECE) <= 8
            and width % TILE == 0
            and features % TILE == 0
            and tokens.shape[1] * width <= 2 ** 21
            and width * features <= 2 ** 21
        )
        if fits:
            return fused(n_row, tokens, w_gate, w_up, w_down)
        return plain(tokens, w_gate, w_up, w_down)

    in_specs = (P(None, "col"), P("col", "row"), P("col", "row"), P("row", "col"))
    return jax.shard_map(local, mesh=mesh, in_specs=in_specs, out_specs=P("row", "col"), check_vma=False)
```

time: 141 us -> 53.8 us (0.38)
  waiting for transfers between devices: 107 us -> 0 us
  Pallas kernels: 0 us -> 50 us
  between operations: 13.1 us -> 0.01 us
  matrix products: 11.6 us -> 0 us
  other arithmetic: 2.66 us -> 0 us
  local copies, waits for them, and re-layouts: 5.79 us -> 3.62 us
    pallas_call x0 -> x1, Pallas kernels: none -> 50 us  [fused(): pl.pallas_call(functools.partial(kernel, n_row, chunks), out_shape=jax.Sh...]
    unnamed x4 -> x0, waiting for transfers between devices: 42.4 us -> none
    reduce_scatter x1 -> x0, waiting for transfers between devices: 36.2 us -> none  [local(): lax.psum_scatter(jnp.dot(hidden_all, w_down, preferred_element_type=jnp.f...]
    all_gather x1 -> x0, waiting for transfers between devices: 28.6 us -> none  [local(): hidden_all = lax.all_gather(hidden, 'col', axis=0, tiled=True)]
    dot_general x2 -> x0, matrix products: 11.6 us -> none  [the longest x1 7.39 us: local(): jnp.dot(tokens, joined, preferred_element_type=jnp.float32)]
    convert_element_type x3 -> x0, other arithmetic: 2.66 us -> none  [the longest x1 1.62 us: local(): return result.astype(jnp.bfloat16)]
    unnamed x4 -> x5, local copies, waits for them, and re-layouts: 5.79 us -> 3.62 us
  transfers between devices with their start and end apart: 3 -> 0, of which waited for: 3 -> 0; matrix products, arithmetic and copies ran while one was open for 0% -> 0% of each run, Pallas kernels for 0% -> 0%
where the time goes in v1:
time: 53.8 us; the launch traced here: 53.6 us
  Pallas kernels  50 us (93%)
  local copies, waits for them, and re-layouts  3.62 us (7%)
    pallas_call x1, Pallas kernels, fused(): pl.pallas_call(functools.partial(kernel, n_row, chunks), out_shape=jax.Sh...  50 us
    unnamed x5, local copies, waits for them, and re-layouts  3.62 us

profile of v1, /device:TPU:0, one launch (start us, length us, event | category | flops | bytes accessed | tf_op | source)
XLA Modules:
  0.0 53.6 jit_solution(14651410709377511549)
XLA Ops:
  0.0 0.0 copy-start
  0.0 1.7 %copy-done = bf16[1024,1280]{1,0:T(8,128)(2,1)S(1)} copy-done((bf16[1024,1280]{1,0:T(8,128)(2,1)S(1)}, bf16[1024,1280]{1,0:T(8,128)(2,1)}, u32[]{:S(2)}) %copy-start) | copy-done | bytes 2621464
  1.7 0.0 copy-start.1
  1.7 1.2 %copy-done.1 = bf16[512,1024]{1,0:T(8,128)(2,1)S(1)} copy-done((bf16[512,1024]{1,0:T(8,128)(2,1)S(1)}, bf16[512,1024]{1,0:T(8,128)(2,1)}, u32[]{:S(2)}) %copy-start.1) | copy-done | bytes 1048600
  3.0 50.0 %shard_map.46 = bf16[64,1024]{1,0:T(8,128)(2,1)S(1)} custom-call(bf16[2,2,128,1024]{3,2,1,0:T(8,128)(2,1)S(1)} %bitcast.1, bf16[1024,1280]{1,0:T(8,128)(2,1)S(1)} %copy-done, bf16[1024,1280]{1,0:T(8,128)(2,1)} %wu_hbm.1, bf16[1280,1024]{1,0:T(8,128)(2,1)} %wd_hbm.1), custom_call_target="tpu_custom_call" | custom-call | tf_op jit(solution)/shard_map/pallas_call | solution.py:207
  53.0 0.7 %copy.6 = bf16[64,1024]{1,0:T(8,128)(2,1)} copy(bf16[64,1024]{1,0:T(8,128)(2,1)S(1)} %shard_map.46) | data formatting | bytes 262144
Async XLA Ops:
  0.0 1.7 %copy-start = (bf16[1024,1280]{1,0:T(8,128)(2,1)S(1)}, bf16[1024,1280]{1,0:T(8,128)(2,1)}, u32[]{:S(2)}) copy-start(bf16[1024,1280]{1,0:T(8,128)(2,1)} %wg_hbm.1) | copy-start | bytes 7864324
  1.7 1.2 %copy-start.1 = (bf16[512,1024]{1,0:T(8,128)(2,1)S(1)}, bf16[512,1024]{1,0:T(8,128)(2,1)}, u32[]{:S(2)}) copy-start(bf16[512,1024]{1,0:T(8,128)(2,1)} %param.4) | copy-start | bytes 3145732

commit v2 on v1

--- a/solution.py
+++ b/solution.py
@@ -230,7 +230,7 @@
             dma((chunks, n_z - 1)), dma((chunks, n_z - 1)),
         ],
         compiler_params=pltpu.CompilerParams(
-            collective_id=0, has_side_effects=True, vmem_limit_bytes=48 * 1024 * 1024
+            collective_id=0, has_side_effects=True, vmem_limit_bytes=67043328
         ),
     )(tokens.reshape(2, 2, n_tok // 4, depth), w_gate, w_up, w_down)
 

time: 53.8 us -> 52.9 us (0.983)
  local copies, waits for them, and re-layouts: 3.62 us -> 1.57 us
  Pallas kernels: 50 us -> 51.2 us
    unnamed x5 -> x1, local copies, waits for them, and re-layouts: 3.62 us -> 1.57 us
    pallas_call x1, Pallas kernels: 50 us -> 51.2 us  [fused(): pl.pallas_call(functools.partial(kernel, n_row, chunks), out_shape=jax.Sh...]
where the time goes in v2:
time: 52.9 us; the launch traced here: 52.7 us
  Pallas kernels  51.2 us (97%)
  local copies, waits for them, and re-layouts  1.57 us (3%)
    pallas_call x1, Pallas kernels, fused(): pl.pallas_call(functools.partial(kernel, n_row, chunks), out_shape=jax.Sh...  51.2 us
    unnamed x1, local copies, waits for them, and re-layouts  1.57 us

profile of v2, /device:TPU:0, one launch (start us, length us, event | category | flops | bytes accessed | tf_op | source)
XLA Modules:
  0.0 52.7 jit_solution(11018840814739138297)
XLA Ops:
  0.0 51.2 %shard_map.46 = bf16[64,1024]{1,0:T(8,128)(2,1)} custom-call(bf16[2,2,128,1024]{3,2,1,0:T(8,128)(2,1)} %bitcast.1, bf16[1024,1280]{1,0:T(8,128)(2,1)} %wg_hbm.1, bf16[1024,1280]{1,0:T(8,128)(2,1)} %wu_hbm.1, bf16[1280,1024]{1,0:T(8,128)(2,1)} %wd_hbm.1), custom_call_target="tpu_custom_call" | custom-call | tf_op jit(solution)/shard_map/pallas_call | solution.py:207
  51.2 1.6 %copy.6 = bf16[64,1024]{1,0:T(8,128)(2,1)} copy(bf16[64,1024]{1,0:T(8,128)(2,1)} %shard_map.46) | data formatting | bytes 262144

commit v3 on v2

--- a/solution.py
+++ b/solution.py
@@ -8,7 +8,7 @@
 from jax.sharding import PartitionSpec as P
 
 MESH = pl.DeviceIdType.MESH
-PIECE = 16
+PIECE = 8
 TILE = 256
 
 
@@ -37,9 +37,9 @@
 
 
 def kernel(
-    n_row, chunks, tok_hbm, wg_hbm, wu_hbm, wd_hbm, out_ref,
-    tok, w1, wd, s1, own, r1, s2, r2, hid, part, part16, c1r, c2s, c2r,
-    load_sem, send1, recv1, send2, recv2, send3, recv3, send4, recv4, send5, recv5, send6, recv6,
+    n_row, chunks, tok_hbm, wg_hbm, wu_hbm, wd_hbm, out_hbm,
+    tok, w1, wd, s1, own, r1, s2, r2, hid, part, part16, c1r, c2s, c2r, out_ref,
+    load_sem, send1, recv1, send2, recv2, send3, recv3, send4, recv4, send5, recv5, send6, recv6, store_sem,
 ):
     row, col = lax.axis_index("row"), lax.axis_index("col")
     y, x = col // 2, col % 2
@@ -49,7 +49,15 @@
     x_peer = (row, 2 * y + 1 - x)
     y_peer = (row, 2 * (1 - y) + x)
     core_peer = (2 * z + 1 - core, col)
-    z_peers = [(2 * ((z + d) % n_z) + core, col) for d in range(1, n_z)]
+    upper = 2 * z // n_z
+
+    def z_order(k):
+        down = n_z - 1 - k - (z + k + 1) // n_z
+        up = k + (k + n_z - z) // n_z
+        return down * (1 - upper) + up * upper
+
+    z_others = [z_order(k) for k in range(n_z - 1)]
+    z_peers = [(2 * other + core, col) for other in z_others]
     first_peer, second_peer = (x_peer, y_peer), (y_peer, x_peer)
     first_at, second_at = (x, y), (y, x)
 
@@ -91,21 +99,26 @@
     def copy_c1(i):
         return remote(part16.at[i, 1 - core], c1r.at[i], send5.at[i], recv5.at[i], core_peer)
 
-    def copy_c2(i, d):
-        return remote(c2s.at[i, (z + d) % n_z], c2r.at[i, d - 1], send6.at[i, d - 1], recv6.at[i, d - 1], z_peers[d - 1])
-
-    def product(m, mine, dst):
+    def copy_c2(i, k, arriving=False):
+        at = z_others[k] if arriving else z
+        return remote(c2s.at[i, z_others[k]], c2r.at[i, at], send6.at[i, k], recv6.at[i, at], z_peers[k])
+
+    def store(i):
+        rows = pl.ds(i * PIECE, PIECE)
+        return pltpu.make_async_copy(out_ref.at[rows], out_hbm.at[rows], store_sem.at[i])
+
+    def product(m, mine, dst, low, high):
         at = first_at[m] if mine else 1 - first_at[m]
-        rows = tok[:, at] if m == 0 else tok[at]
+        rows = tok[:, at, :, low:high] if m == 0 else tok[at, :, :, low:high]
         rows = rows.reshape(-1, rows.shape[-1])
 
         @pl.loop(0, w1.shape[2] // TILE)
         def _(t):
             columns = pl.ds(pl.multiple_of(t * TILE, TILE), TILE)
             out = jnp.dot(rows, w1[m, :, columns], preferred_element_type=jnp.float32).astype(jnp.bfloat16)
-            out = out.reshape(2, n_row // 4, chunks, PIECE, TILE)
-            for i in range(chunks):
-                dst[m, i, :, :, :, columns] = out[:, :, i]
+            out = out.reshape(2, n_row // 4, high - low, PIECE, TILE)
+            for i in range(low, high):
+                dst[m, i, :, :, :, columns] = out[:, :, i - low]
 
     def f32(v):
         return v.astype(jnp.float32)
@@ -155,30 +168,37 @@
     def do_c2(i):
         copy_c1(i).wait_recv()
         c2s[i] = (part[i, core] + f32(c1r[i])).astype(jnp.bfloat16)
-        for d in range(1, n_z):
-            copy_c2(i, d).start()
+        for k in range(n_z - 1):
+            copy_c2(i, k).start()
 
     def do_out(i):
         total = part[i, core, z] + f32(c1r[i, z])
-        for d in range(1, n_z):
-            copy_c2(i, d).wait_recv()
-            total = total + f32(c2r[i, d - 1])
+        for k in reversed(range(n_z - 1)):
+            copy_c2(i, k, True).wait_recv()
+            total = total + f32(c2r[i, z_others[k]])
         out_ref[pl.ds(i * PIECE, PIECE), :] = total.astype(jnp.bfloat16)
-
+        store(i).start()
+
+    first = max(chunks // 4, 1)
+    ahead = min(4, chunks)
     for load in loads[:3]:
         load.wait()
-    product(0, False, s1)
+    product(0, False, s1, 0, first)
     pl.semaphore_wait(barrier, len(peers))
-    ahead = min(2, chunks)
-    for i in range(ahead):
+    for i in range(first):
         copy_s1(0, i).start()
     for load in loads[3:5]:
         load.wait()
-    product(1, False, s1)
-    for i in range(ahead):
+    product(1, False, s1, 0, first)
+    for i in range(first):
         copy_s1(1, i).start()
-    product(0, True, own)
-    product(1, True, own)
+    for m in range(2):
+        if first < chunks:
+            product(m, False, s1, first, chunks)
+            for i in range(first, ahead):
+                copy_s1(m, i).start()
+    product(0, True, own, 0, chunks)
+    product(1, True, own, 0, chunks)
     loads[5].wait()
 
     for k in range(chunks + 6):
@@ -192,8 +212,9 @@
             for copy in (copy_s1, copy_s2, copy_g1, copy_g2):
                 copy(m, i).wait_send()
         copy_c1(i).wait_send()
-        for d in range(1, n_z):
-            copy_c2(i, d).wait_send()
+        for k in range(n_z - 1):
+            copy_c2(i, k).wait_send()
+        store(i).wait()
 
 
 def fused(n_row, tokens, w_gate, w_up, w_down):
@@ -208,9 +229,9 @@
         functools.partial(kernel, n_row, chunks),
         out_shape=jax.ShapeDtypeStruct((per_row, features), bf16),
         in_specs=[pl.BlockSpec(memory_space=pl.ANY)] * 4,
-        out_specs=pl.BlockSpec(memory_space=pltpu.VMEM),
+        out_specs=pl.BlockSpec(memory_space=pl.ANY),
         scratch_shapes=[
-            pltpu.VMEM((2, 2, n_tok // 4, depth), bf16),
+            pltpu.VMEM((2, 2, blocks, chunks, PIECE, depth), bf16),
             pltpu.VMEM((2, depth, width), bf16),
             pltpu.VMEM((width, features), bf16),
             pltpu.VMEM((2, chunks, 2, blocks, PIECE, width), bf16),
@@ -223,16 +244,17 @@
             pltpu.VMEM((chunks, 2, n_z, PIECE, features), bf16),
             pltpu.VMEM((chunks, n_z, PIECE, features), bf16),
             pltpu.VMEM((chunks, n_z, PIECE, features), bf16),
-            pltpu.VMEM((chunks, n_z - 1, PIECE, features), bf16),
+            pltpu.VMEM((chunks, n_z, PIECE, features), bf16),
+            pltpu.VMEM((per_row, features), bf16),
             dma((6,)),
             *pair,
             dma((chunks,)), dma((chunks,)),
-            dma((chunks, n_z - 1)), dma((chunks, n_z - 1)),
+            dma((chunks, n_z - 1)), dma((chunks, n_z)), dma((chunks,)),
         ],
         compiler_params=pltpu.CompilerParams(
             collective_id=0, has_side_effects=True, vmem_limit_bytes=67043328
         ),
-    )(tokens.reshape(2, 2, n_tok // 4, depth), w_gate, w_up, w_down)
+    )(tokens.reshape(2, 2, blocks, chunks, PIECE, depth), w_gate, w_up, w_down)
 
 
 def solution(mesh):
@@ -245,7 +267,7 @@
             and n_row % 4 == 0
             and n_row <= 16
             and tokens.shape[0] % (n_row * PIECE) == 0
-            and tokens.shape[0] // (n_row * PIECE) <= 8
+            and tokens.shape[0] // (n_row * PIECE) <= 16
             and width % TILE == 0
             and features % TILE == 0
             and tokens.shape[1] * width <= 2 ** 21

time: 52.9 us -> 55.3 us (1.045)
  Pallas kernels: 51.2 us -> 53.5 us
    pallas_call x1, Pallas kernels: 51.2 us -> 53.5 us  [fused(): pl.pallas_call(functools.partial(kernel, n_row, chunks), out_shape=jax.Sh...]
where the time goes in v3:
time: 55.3 us; the launch traced here: 55.1 us
  Pallas kernels  53.5 us (97%)
  local copies, waits for them, and re-layouts  1.57 us (3%)
    pallas_call x1, Pallas kernels, fused(): pl.pallas_call(functools.partial(kernel, n_row, chunks), out_shape=jax.Sh...  53.5 us
    unnamed x1, local copies, waits for them, and re-layouts  1.57 us

profile of v3, /device:TPU:0, one launch (start us, length us, event | category | flops | bytes accessed | tf_op | source)
XLA Modules:
  0.0 55.1 jit_solution(17556627382454058562)
XLA Ops:
  0.0 53.5 %shard_map.46 = bf16[64,1024]{1,0:T(8,128)(2,1)} custom-call(bf16[2,2,2,8,8,1024]{5,4,3,2,1,0:T(8,128)(2,1)} %bitcast.1, bf16[1024,1280]{1,0:T(8,128)(2,1)} %wg_hbm.1, bf16[1024,1280]{1,0:T(8,128)(2,1)} %wu_hbm.1, bf16[1280,1024]{1,0:T(8,128)(2,1)} %wd_hbm.1), custom_call_target="tpu_custom_call" | custom-call | tf_op jit(solution)/shard_map/pallas_call | solution.py:228
  53.6 1.6 %copy.6 = bf16[64,1024]{1,0:T(8,128)(2,1)} copy(bf16[64,1024]{1,0:T(8,128)(2,1)} %shard_map.46) | data formatting | bytes 262144

commit v4 on v3

v4 whole, which is shorter than its diff:
```python
import functools

import jax
import jax.numpy as jnp
from jax import lax
from jax.experimental import pallas as pl
from jax.experimental.pallas import tpu as pltpu
from jax.sharding import PartitionSpec as P

MESH = pl.DeviceIdType.MESH
PIECE = 8
TILE = 256


def activate(pre_gate, pre_up):
    return (jax.nn.gelu(pre_gate, approximate=True) * pre_up).astype(jnp.bfloat16)


def plain(tokens, w_gate, w_up, w_down):
    joined = jnp.concatenate([w_gate, w_up], axis=1)
    hidden_width = w_gate.shape[1]
    summed = lax.psum_scatter(
        jnp.dot(tokens, joined, preferred_element_type=jnp.float32).astype(jnp.bfloat16),
        "col",
        scatter_dimension=0,
        tiled=True,
    ).astype(jnp.float32)
    hidden = activate(summed[:, :hidden_width], summed[:, hidden_width:])
    hidden_all = lax.all_gather(hidden, "col", axis=0, tiled=True)
    result = lax.psum_scatter(
        jnp.dot(hidden_all, w_down, preferred_element_type=jnp.float32),
        "row",
        scatter_dimension=0,
        tiled=True,
    )
    return result.astype(jnp.bfloat16)


def chunk_rows(per_row):
    units = per_row // PIECE
    base = max(units // 4, 1)
    sizes = [base] * (units // base)
    sizes[0] += units - sum(sizes)
    if len(sizes) > 1 and base > 1:
        sizes[0] += base // 2
        sizes[-1] -= base // 2
    return [size * PIECE for size in sizes]


def kernel(
    n_row, sizes, tok_hbm, wg_hbm, wu_hbm, wd_hbm, out_hbm,
    tok, w1, wd, s1, own, r1, s2, r2, hid, part, part16, c1r, c2s, c2r, out_ref,
    load_sem, send1, recv1, send2, recv2, send3, recv3, send4, recv4, send5, recv5, send6, recv6, store_sem,
):
    row, col = lax.axis_index("row"), lax.axis_index("col")
    y, x = col // 2, col % 2
    z, core = row // 2, row % 2
    n_z = n_row // 2
    chunks = len(sizes)
    spans = [pl.ds(sum(sizes[:i]), sizes[i]) for i in range(chunks)]
    half = w1.shape[2] // 2
    x_peer = (row, 2 * y + 1 - x)
    y_peer = (row, 2 * (1 - y) + x)
    core_peer = (2 * z + 1 - core, col)
    upper = 2 * z // n_z

    def z_order(k):
        down = n_z - 1 - k - (z + k + 1) // n_z
        up = k + (k + n_z - z) // n_z
        return down * (1 - upper) + up * upper

    z_others = [z_order(k) for k in range(n_z - 1)]
    z_peers = [(2 * other + core, col) for other in z_others]
    first_peer, second_peer = (x_peer, y_peer), (y_peer, x_peer)
    first_at, second_at = (x, y), (y, x)

    loads = [pltpu.make_async_copy(tok_hbm, tok, load_sem.at[0])]
    for mode in range(2):
        for k, w_hbm in enumerate((wg_hbm, wu_hbm)):
            loads.append(pltpu.make_async_copy(
                w_hbm.at[:, pl.ds(mode * half, half)],
                w1.at[mode, :, pl.ds(k * half, half)],
                load_sem.at[1 + 2 * mode + k],
            ))
    loads.append(pltpu.make_async_copy(wd_hbm, wd, load_sem.at[5]))
    for load in loads[:3]:
        load.start()

    barrier = pltpu.get_barrier_semaphore()
    peers = [x_peer, y_peer, core_peer] + z_peers
    for peer in peers:
        pl.semaphore_signal(barrier, inc=1, device_id=peer, device_id_type=MESH)

    def remote(src, dst, send_sem, recv_sem, peer):
        return pltpu.make_async_remote_copy(
            src_ref=src, dst_ref=dst, send_sem=send_sem, recv_sem=recv_sem, device_id=peer, device_id_type=MESH)

    def copy_s1(m, i):
        return remote(s1.at[m, :, :, spans[i]], r1.at[m, :, :, spans[i]], send1.at[m, i], recv1.at[m, i], first_peer[m])

    def copy_s2(m, i):
        return remote(s2.at[m, :, spans[i]], r2.at[m, :, spans[i]], send2.at[m, i], recv2.at[m, i], second_peer[m])

    def copy_g1(m, i):
        ref = hid.at[m, first_at[m], second_at[m], :, spans[i]]
        return remote(ref, ref, send3.at[m, i], recv3.at[m, i], second_peer[m])

    def copy_g2(m, i):
        ref = hid.at[m, first_at[m], :, :, spans[i]]
        return remote(ref, ref, send4.at[m, i], recv4.at[m, i], first_peer[m])

    def copy_c1(i):
        return remote(part16.at[1 - core, :, spans[i]], c1r.at[:, spans[i]], send5.at[i], recv5.at[i], core_peer)

    def copy_c2(i, k, arriving=False):
        at = z_others[k] if arriving else z
        return remote(c2s.at[z_others[k], spans[i]], c2r.at[at, spans[i]], send6.at[i, k], recv6.at[i, at], z_peers[k])

    def store(i):
        return pltpu.make_async_copy(out_ref.at[spans[i]], out_hbm.at[spans[i]], store_sem.at[i])

    def product(m, mine, dst):
        at = first_at[m] if mine else 1 - first_at[m]
        rows = tok[:, at] if m == 0 else tok[at]
        shape = rows.shape[:-1]
        rows = rows.reshape(-1, rows.shape[-1])
        for t in range(w1.shape[2] // TILE):
            columns = slice(t * TILE, (t + 1) * TILE)
            out = jnp.dot(rows, w1[m, :, columns], preferred_element_type=jnp.float32)
            dst[m, :, :, :, columns] = out.astype(jnp.bfloat16).reshape(*shape, TILE)

    def f32(v):
        return v.astype(jnp.float32)

    def do_s1(i):
        for m in range(2):
            copy_s1(m, i).start()

    def do_s2(i):
        for m in range(2):
            copy_s1(m, i).wait_recv()
            at, span = 1 - second_at[m], spans[i]
            s2[m, :, span] = (f32(own[m, at, :, span]) + f32(r1[m, at, :, span])).astype(jnp.bfloat16)
            copy_s2(m, i).start()

    def do_g1(i):
        for m in range(2):
            copy_s2(m, i).wait_recv()
            at, span = second_at[m], spans[i]
            pre = f32(own[m, at, :, span]) + f32(r1[m, at, :, span]) + f32(r2[m, :, span])
            hid[m, first_at[m], at, :, span] = activate(pre[..., :half], pre[..., half:])
            copy_g1(m, i).start()

    def do_g2(i):
        for m in range(2):
            copy_g1(m, i).wait_recv()
            copy_g2(m, i).start()

    def do_c1(i):
        for m in range(2):
            copy_g2(m, i).wait_recv()
        span = spans[i]
        rows = n_row // 4 * sizes[i]
        quarters = [
            jnp.concatenate([hid[0, b, a, :, span].reshape(rows, half), hid[1, a, b, :, span].reshape(rows, half)], axis=1)
            for a in range(2) for b in range(2)
        ]
        hidden = jnp.concatenate(quarters, axis=0)
        for t in range(wd.shape[1] // TILE):
            columns = slice(t * TILE, (t + 1) * TILE)
            out = jnp.dot(hidden, wd[:, columns], preferred_element_type=jnp.float32)
            out = out.reshape(n_z, 2, sizes[i], TILE)
            for c in range(2):
                part[c, :, span, columns] = out[:, c]
                part16[c, :, span, columns] = out[:, c].astype(jnp.bfloat16)
        copy_c1(i).start()

    def do_c2(i):
        copy_c1(i).wait_recv()
        span = spans[i]
        c2s[:, span] = (part[core, :, span] + f32(c1r[:, span])).astype(jnp.bfloat16)
        for k in range(n_z - 1):
            copy_c2(i, k).start()

    def do_out(i):
        span = spans[i]
        total = part[core, z, span] + f32(c1r[z, span])
        for k in reversed(range(n_z - 1)):
            copy_c2(i, k, True).wait_recv()
            total = total + f32(c2r[z_others[k], span])
        out_ref[span] = total.astype(jnp.bfloat16)
        store(i).start()

    ahead = min(2, chunks)
    loads[0].wait()
    for load in loads[3:]:
        load.start()
    for load in loads[1:3]:
        load.wait()
    product(0, False, s1)
    pl.semaphore_wait(barrier, len(peers))
    for i in range(ahead):
        copy_s1(0, i).start()
    for load in loads[3:5]:
        load.wait()
    product(1, False, s1)
    for i in range(ahead):
        copy_s1(1, i).start()
    product(0, True, own)
    product(1, True, own)
    loads[5].wait()

    for k in range(chunks + 6):
        for stage, late in ((do_s2, 0), (do_g1, 1), (do_s1, -2), (do_g2, 2), (do_c2, 4), (do_c1, 3), (do_out, 6)):
            i = k - late
            if 0 <= i < chunks and (stage is not do_s1 or i >= ahead):
                stage(i)

    for i in range(chunks):
        for m in range(2):
            for copy in (copy_s1, copy_s2, copy_g1, copy_g2):
                copy(m, i).wait_send()
        copy_c1(i).wait_send()
        for k in range(n_z - 1):
            copy_c2(i, k).wait_send()
        store(i).wait()


def fused(n_row, tokens, w_gate, w_up, w_down):
    n_tok, depth = tokens.shape
    width, features = w_down.shape
    per_row = n_tok // n_row
    sizes = chunk_rows(per_row)
    chunks = len(sizes)
    n_z, blocks, half = n_row // 2, n_row // 4, width // 2
    bf16, dma = jnp.bfloat16, pltpu.SemaphoreType.DMA
    pair = [dma((2, chunks))] * 8
    return pl.pallas_call(
        functools.partial(kernel, n_row, sizes),
        out_shape=jax.ShapeDtypeStruct((per_row, features), bf16),
        in_specs=[pl.BlockSpec(memory_space=pl.ANY)] * 4,
        out_specs=pl.BlockSpec(memory_space=pl.ANY),
        scratch_shapes=[
            pltpu.VMEM((2, 2, blocks, per_row, depth), bf16),
            pltpu.VMEM((2, depth, width), bf16),
            pltpu.VMEM((width, features), bf16),
            pltpu.VMEM((2, 2, blocks, per_row, width), bf16),
            pltpu.VMEM((2, 2, blocks, per_row, width), bf16),
            pltpu.VMEM((2, 2, blocks, per_row, width), bf16),
            pltpu.VMEM((2, blocks, per_row, width), bf16),
            pltpu.VMEM((2, blocks, per_row, width), bf16),
            pltpu.VMEM((2, 2, 2, blocks, per_row, half), bf16),
            pltpu.VMEM((2, n_z, per_row, features), jnp.float32),
            pltpu.VMEM((2, n_z, per_row, features), bf16),
            pltpu.VMEM((n_z, per_row, features), bf16),
            pltpu.VMEM((n_z, per_row, features), bf16),
            pltpu.VMEM((n_z, per_row, features), bf16),
            pltpu.VMEM((per_row, features), bf16),
            dma((6,)),
            *pair,
            dma((chunks,)), dma((chunks,)),
            dma((chunks, n_z - 1)), dma((chunks, n_z)), dma((chunks,)),
        ],
        compiler_params=pltpu.CompilerParams(
            collective_id=0, has_side_effects=True, vmem_limit_bytes=67043328
        ),
    )(tokens.reshape(2, 2, blocks, per_row, depth), w_gate, w_up, w_down)


def solution(mesh):
    n_row, n_col = mesh.shape["row"], mesh.shape["col"]

    def local(tokens, w_gate, w_up, w_down):
        width, features = w_down.shape
        fits = (
            n_col == 4
            and n_row % 4 == 0
            and n_row <= 16
            and tokens.shape[0] % (n_row * PIECE) == 0
            and tokens.shape[0] // (n_row * PIECE) <= 16
            and width % TILE == 0
            and features % TILE == 0
            and tokens.shape[1] * width <= 2 ** 21
            and width * features <= 2 ** 21
        )
        if fits:
            return fused(n_row, tokens, w_gate, w_up, w_down)
        return plain(tokens, w_gate, w_up, w_down)

    in_specs = (P(None, "col"), P("col", "row"), P("col", "row"), P("row", "col"))
    return jax.shard_map(local, mesh=mesh, in_specs=in_specs, out_specs=P("row", "col"), check_vma=False)
```

time: 55.3 us -> 53.6 us (0.969)
  Pallas kernels: 53.5 us -> 51.9 us
    pallas_call x1, Pallas kernels: 53.5 us -> 51.9 us  [fused(): pl.pallas_call(functools.partial(kernel, n_row, sizes), out_shape=jax.Sha...]
where the time goes in v4:
time: 53.6 us; the launch traced here: 53.5 us
  Pallas kernels  51.9 us (97%)
  local copies, waits for them, and re-layouts  1.57 us (3%)
    pallas_call x1, Pallas kernels, fused(): pl.pallas_call(functools.partial(kernel, n_row, sizes), out_shape=jax.Sha...  51.9 us
    unnamed x1, local copies, waits for them, and re-layouts  1.57 us

profile of v4, /device:TPU:0, one launch (start us, length us, event | category | flops | bytes accessed | tf_op | source)
XLA Modules:
  0.0 53.5 jit_solution(18335426835846396469)
XLA Ops:
  0.0 51.9 %shard_map.46 = bf16[64,1024]{1,0:T(8,128)(2,1)} custom-call(bf16[2,2,2,64,1024]{4,3,2,1,0:T(8,128)(2,1)} %bitcast.1, bf16[1024,1280]{1,0:T(8,128)(2,1)} %wg_hbm.1, bf16[1024,1280]{1,0:T(8,128)(2,1)} %wu_hbm.1, bf16[1280,1024]{1,0:T(8,128)(2,1)} %wd_hbm.1), custom_call_target="tpu_custom_call" | custom-call | tf_op jit(solution)/shard_map/pallas_call | solution.py:238
  51.9 1.6 %copy.6 = bf16[64,1024]{1,0:T(8,128)(2,1)} copy(bf16[64,1024]{1,0:T(8,128)(2,1)} %shard_map.46) | data formatting | bytes 262144

commit v5 on v4

--- a/solution.py
+++ b/solution.py
@@ -38,13 +38,8 @@
 
 def chunk_rows(per_row):
     units = per_row // PIECE
-    base = max(units // 4, 1)
-    sizes = [base] * (units // base)
-    sizes[0] += units - sum(sizes)
-    if len(sizes) > 1 and base > 1:
-        sizes[0] += base // 2
-        sizes[-1] -= base // 2
-    return [size * PIECE for size in sizes]
+    sizes = [1, 1, 2, 2, 1, 1] if units % 8 == 0 else [1] * units
+    return [size * per_row // sum(sizes) for size in sizes]
 
 
 def kernel(
@@ -119,15 +114,15 @@
     def store(i):
         return pltpu.make_async_copy(out_ref.at[spans[i]], out_hbm.at[spans[i]], store_sem.at[i])
 
-    def product(m, mine, dst):
+    def product(m, mine, dst, low, high):
         at = first_at[m] if mine else 1 - first_at[m]
-        rows = tok[:, at] if m == 0 else tok[at]
+        rows = tok[:, at, :, low:high] if m == 0 else tok[at, :, :, low:high]
         shape = rows.shape[:-1]
         rows = rows.reshape(-1, rows.shape[-1])
         for t in range(w1.shape[2] // TILE):
             columns = slice(t * TILE, (t + 1) * TILE)
             out = jnp.dot(rows, w1[m, :, columns], preferred_element_type=jnp.float32)
-            dst[m, :, :, :, columns] = out.astype(jnp.bfloat16).reshape(*shape, TILE)
+            dst[m, :, :, low:high, columns] = out.astype(jnp.bfloat16).reshape(*shape, TILE)
 
     def f32(v):
         return v.astype(jnp.float32)
@@ -191,30 +186,35 @@
         out_ref[span] = total.astype(jnp.bfloat16)
         store(i).start()
 
-    ahead = min(2, chunks)
+    first, ahead = min(2, chunks), min(3, chunks)
+    cut, end = sum(sizes[:first]), sum(sizes)
     loads[0].wait()
     for load in loads[3:]:
         load.start()
-    for load in loads[1:3]:
-        load.wait()
-    product(0, False, s1)
-    pl.semaphore_wait(barrier, len(peers))
-    for i in range(ahead):
-        copy_s1(0, i).start()
-    for load in loads[3:5]:
-        load.wait()
-    product(1, False, s1)
-    for i in range(ahead):
-        copy_s1(1, i).start()
-    product(0, True, own)
-    product(1, True, own)
+    for m in range(2):
+        for load in loads[1 + 2 * m:3 + 2 * m]:
+            load.wait()
+        product(m, False, s1, 0, cut)
+        if m == 0:
+            pl.semaphore_wait(barrier, len(peers))
+        for i in range(first):
+            copy_s1(m, i).start()
+    for m in range(2):
+        if cut < end:
+            product(m, False, s1, cut, end)
+            for i in range(first, ahead):
+                copy_s1(m, i).start()
+    for m in range(2):
+        product(m, True, own, 0, end)
     loads[5].wait()
 
-    for k in range(chunks + 6):
-        for stage, late in ((do_s2, 0), (do_g1, 1), (do_s1, -2), (do_g2, 2), (do_c2, 4), (do_c1, 3), (do_out, 6)):
+    for k in range(chunks + 4):
+        for stage, late in ((do_s2, 0), (do_g1, 1), (do_s1, -2), (do_g2, 2), (do_c2, 4), (do_c1, 3)):
             i = k - late
             if 0 <= i < chunks and (stage is not do_s1 or i >= ahead):
                 stage(i)
+    for i in range(chunks):
+        do_out(i)
 
     for i in range(chunks):
         for m in range(2):

time: 53.6 us -> 52.2 us (0.974)
  Pallas kernels: 51.9 us -> 50.5 us
    pallas_call x1, Pallas kernels: 51.9 us -> 50.5 us  [fused(): pl.pallas_call(functools.partial(kernel, n_row, sizes), out_shape=jax.Sha...]
where the time goes in v5:
time: 52.2 us; the launch traced here: 52.1 us
  Pallas kernels  50.5 us (97%)
  local copies, waits for them, and re-layouts  1.57 us (3%)
    pallas_call x1, Pallas kernels, fused(): pl.pallas_call(functools.partial(kernel, n_row, sizes), out_shape=jax.Sha...  50.5 us
    unnamed x1, local copies, waits for them, and re-layouts  1.57 us

profile of v5, /device:TPU:0, one launch (start us, length us, event | category | flops | bytes accessed | tf_op | source)
XLA Modules:
  0.0 52.1 jit_solution(10293719150209330892)
XLA Ops:
  0.0 50.5 %shard_map.46 = bf16[64,1024]{1,0:T(8,128)(2,1)} custom-call(bf16[2,2,2,64,1024]{4,3,2,1,0:T(8,128)(2,1)} %bitcast.1, bf16[1024,1280]{1,0:T(8,128)(2,1)} %wg_hbm.1, bf16[1024,1280]{1,0:T(8,128)(2,1)} %wu_hbm.1, bf16[1280,1024]{1,0:T(8,128)(2,1)} %wd_hbm.1), custom_call_target="tpu_custom_call" | custom-call | tf_op jit(solution)/shard_map/pallas_call | solution.py:238
  50.5 1.6 %copy.6 = bf16[64,1024]{1,0:T(8,128)(2,1)} copy(bf16[64,1024]{1,0:T(8,128)(2,1)} %shard_map.46) | data formatting | bytes 262144

commit v6 on v5

--- a/solution.py
+++ b/solution.py
@@ -209,7 +209,7 @@
     loads[5].wait()
 
     for k in range(chunks + 4):
-        for stage, late in ((do_s2, 0), (do_g1, 1), (do_s1, -2), (do_g2, 2), (do_c2, 4), (do_c1, 3)):
+        for stage, late in ((do_s2, 0), (do_g1, 1), (do_s1, -3), (do_g2, 2), (do_c2, 4), (do_c1, 3)):
             i = k - late
             if 0 <= i < chunks and (stage is not do_s1 or i >= ahead):
                 stage(i)

time: 52.2 us -> 51.8 us (level)
  no operation moved by 1% of the time
where the time goes in v6:
time: 51.8 us; the launch traced here: 51.7 us
  Pallas kernels  50.1 us (97%)
  local copies, waits for them, and re-layouts  1.57 us (3%)
    pallas_call x1, Pallas kernels, fused(): pl.pallas_call(functools.partial(kernel, n_row, sizes), out_shape=jax.Sha...  50.1 us
    unnamed x1, local copies, waits for them, and re-layouts  1.57 us

profile of v6, /device:TPU:0, one launch (start us, length us, event | category | flops | bytes accessed | tf_op | source)
XLA Modules:
  0.0 51.7 jit_solution(11281732780789102620)
XLA Ops:
  0.0 50.1 %shard_map.46 = bf16[64,1024]{1,0:T(8,128)(2,1)} custom-call(bf16[2,2,2,64,1024]{4,3,2,1,0:T(8,128)(2,1)} %bitcast.1, bf16[1024,1280]{1,0:T(8,128)(2,1)} %wg_hbm.1, bf16[1024,1280]{1,0:T(8,128)(2,1)} %wu_hbm.1, bf16[1280,1024]{1,0:T(8,128)(2,1)} %wd_hbm.1), custom_call_target="tpu_custom_call" | custom-call | tf_op jit(solution)/shard_map/pallas_call | solution.py:238
  50.1 1.6 %copy.6 = bf16[64,1024]{1,0:T(8,128)(2,1)} copy(bf16[64,1024]{1,0:T(8,128)(2,1)} %shard_map.46) | data formatting | bytes 262144
